TPU v7x, 128 devices: a whole 4x4x4 slice. The times are simulated.
128 devices in a mesh: cx: 8 (over y, core), cy: 16 (over z, x).
Axes of the slice: x: 4, y: 4, z: 4, core: 2. Of those that a mesh axis runs over, the one named last changes fastest.
Arguments:
- queries: bfloat16 [24576, 4096], P(('cx', 'cy')), may hold values from -300 to 300
- keys: bfloat16 [131072, 512], P(('cx', 'cy')), may hold values from -6 to 6
- values: bfloat16 [131072, 512], P(('cx', 'cy')), may hold values from -6 to 6
- d_out: bfloat16 [24576, 4096], P(('cx', 'cy')), may hold values from -6 to 6
- selection: int32 [384, 4, 16], replicated, may hold values from 0 to 1663, as said below
Outputs:
- d_queries: float32 [24576, 4096], P(('cx', 'cy'))
- d_keys: float32 [131072, 512], P(('cx', 'cy'))
- d_values: float32 [131072, 512], P(('cx', 'cy'))
Inputs may be any that keep to these rules, and one draw needn't show every extreme that they name: `selection`: every entry is a block below 1664. Over the 3 consecutive query blocks of one device (rows d * 3 to d * 3 + 2) all 192 entries differ, and at most 2 of them lie in the blocks k * 16 to k * 16 + 15 of any one k; that most is reached on every device.
All inputs are finite; a program needn't handle non-finite values.
Results may differ from a plain program's by a relative error of at most 0.0042.
Values may be sent and summed in bfloat16 or wider, within the bound.
A program may use at most 192 MiB of HBM per device.

v0:
```python
import jax
import jax.numpy as jnp
from jax import lax
from jax.experimental import pallas as pl
from jax.experimental.pallas import tpu as pltpu
from jax.sharding import PartitionSpec as P

H = 32
KVH = 4
HD = 128
BLK = 64
TOPK = 16
QB_DEV = 3
KB_DEV = 16
GROUP = 8
PICKS = 192
CAP = 2
DEVICES = 128
VALID = DEVICES * (KB_DEV - QB_DEV) // KB_DEV
SLOTS = VALID * CAP
TILES = KB_DEV * KVH
SETS = QB_DEV * KVH
KEYS = TOPK * BLK
ROWS = GROUP * BLK
CHUNK = 256
CHUNKS = KEYS // CHUNK
UNROLL = True
SCALE = HD**-0.5
EXP2_SCALE = SCALE * 1.4426950408889634
MESH = pl.DeviceIdType.MESH
MIB = 1024 * 1024


def fill_tables(me, picks, tile_of, pick_of, chosen):
    rows = lax.broadcasted_iota(jnp.int32, (DEVICES, PICKS), 0)
    chosen[...] = jnp.sum(jnp.where(rows == me, picks, 0), axis=0, keepdims=True)
    shape = (PICKS, DEVICES)
    position = lax.broadcasted_iota(jnp.int32, shape, 0)
    device = lax.broadcasted_iota(jnp.int32, shape, 1)
    block = picks.T
    mine = block // KB_DEV == me
    code = position * TILES + block % KB_DEV * KVH + position // TOPK % KVH
    big = PICKS * TILES
    first = jnp.min(jnp.where(mine, code, big), axis=0, keepdims=True)
    last = jnp.max(jnp.where(mine, code, -1), axis=0, keepdims=True)
    tile_of[0:1, :] = jnp.where(first < big, first % TILES, TILES)
    tile_of[1:2, :] = jnp.where(last > first, last % TILES, TILES)
    own = jnp.sum(jnp.where(device == me, block, 0), axis=1, keepdims=True)
    held = own // KB_DEV == device
    pick_of[0:1, :] = jnp.min(jnp.where(held, position, PICKS - 1), axis=0, keepdims=True)
    pick_of[1:2, :] = jnp.max(jnp.where(held, position, 0), axis=0, keepdims=True)


STRIDES = [(a, b) for b in range(4) for a in range(4)]
ROUNDS = DEVICES // len(STRIDES)


def exchange_kernel(
    picks_hbm, q_hbm, k_hbm, v_hbm, o_hbm,
    dq_hbm, gk_hbm, gv_hbm, tile_hbm,
    picks, tile_v, pick_v, chosen_v, tile_of, pick_of, chosen,
    kl, vl, sendk, sendv, rk, rv, q_s, o_s, e_s, inv_s, dp_s, kg, vg, qg, og,
    terms, dq_acc, dq_s,
    load_sem, send_sem, recv_sem, own_sem,
):
    cx, cy = lax.axis_index("cx"), lax.axis_index("cy")
    me = cx * 16 + cy
    at_x = [(cy + a) % 4 for a in range(4)]
    at_z = [(cy // 4 + b) % 4 * 4 for b in range(4)]

    def peers(turn):
        core = (cx + turn // 4) % 2
        y = [(cx // 2 + turn % 4 + e) % 4 * 2 + core for e in range(4)]
        return [(y[(a + b) % 4], at_z[(a + b) % 4] + at_x[a]) for a, b in STRIDES]

    def load_tiles(src, dst, sem):
        def body(t, carry):
            rows = pl.ds(pl.multiple_of(t // KVH * BLK, BLK), BLK)
            lanes = pl.ds(pl.multiple_of(t % KVH * HD, HD), HD)
            pltpu.make_async_copy(src.at[rows, lanes], dst.at[t], sem).start()
            return carry

        lax.fori_loop(0, TILES, body, 0)

    def wait_bytes(ref, sem):
        pltpu.make_async_copy(ref, ref, sem).wait()

    def greet(turn, carry):
        for n, device in enumerate(peers(turn)):

            @pl.when((turn > 0) | (n > 0))
            def _():
                pl.semaphore_signal(barrier, inc=1, device_id=device, device_id_type=MESH)

        return carry

    barrier = pltpu.get_barrier_semaphore()
    load_picks = pltpu.make_async_copy(picks_hbm, picks, load_sem.at[4])
    load_picks.start()
    lax.fori_loop(0, ROUNDS, greet, 0)
    load_tiles(k_hbm, kl, load_sem.at[0])
    load_tiles(v_hbm, vl, load_sem.at[1])
    load_q = pltpu.make_async_copy(q_hbm, q_s, load_sem.at[2])
    load_o = pltpu.make_async_copy(o_hbm, o_s, load_sem.at[3])
    load_q.start()
    load_o.start()
    load_picks.wait()
    fill_tables(me, picks[...], tile_v, pick_v, chosen_v)
    moves = [
        pltpu.make_async_copy(tile_v, tile_of, load_sem.at[4]),
        pltpu.make_async_copy(pick_v, pick_of, load_sem.at[5]),
        pltpu.make_async_copy(chosen_v, chosen, load_sem.at[6]),
        pltpu.make_async_copy(tile_v, tile_hbm, load_sem.at[7]),
    ]
    for move in moves:
        move.start()

    def forward_copy(send, got, index, device):
        return pltpu.make_async_remote_copy(
            src_ref=send.at[pl.ds(CAP * (device[0] * 16 + device[1]), CAP)],
            dst_ref=got.at[pl.ds(CAP * me, CAP)],
            send_sem=send_sem.at[index],
            recv_sem=recv_sem.at[index],
            device_id=device,
            device_id_type=MESH,
        )

    def forward(local, send, got, index):
        @pl.when(me < VALID)
        def _():
            for c in range(CAP):
                tile = jnp.minimum(tile_of[c, me], TILES - 1)
                got[me * CAP + c] = local[tile]

            def body(turn, carry):
                devices = peers(turn)
                for a, b in devices:
                    for c in range(CAP):
                        tile = jnp.minimum(tile_of[c, a * 16 + b], TILES - 1)
                        send[(a * 16 + b) * CAP + c] = local[tile]
                for n, device in enumerate(devices):

                    @pl.when((turn > 0) | (n > 0))
                    def _():
                        forward_copy(send, got, index, device).start()

                return carry

            lax.fori_loop(0, ROUNDS, body, 0)

    def wait_forward(got, index):
        @pl.when(me < VALID)
        def _():
            wait_bytes(got.at[pl.ds(0, SLOTS - CAP)], recv_sem.at[index])

        @pl.when(me >= VALID)
        def _():
            wait_bytes(got, recv_sem.at[index])

    def gather(got, dst, group):
        def body(j, carry):
            rows = pl.ds(pl.multiple_of(j * BLK, BLK), BLK)
            owner = chosen[0, group * TOPK + j] // KB_DEV
            later = (pick_of[0, owner] != group * TOPK + j).astype(jnp.int32)
            dst[rows, :] = got[owner * CAP + later]
            return carry

        lax.fori_loop(0, TOPK, body, 0)

    def rows_of(src, dst, group):
        b, g = group // KVH, group % KVH
        rows = pl.ds(pl.multiple_of(b * BLK, BLK), BLK)
        for h in range(GROUP):
            lanes = pl.ds(pl.multiple_of((g * GROUP + h) * HD, HD), HD)
            dst[h * BLK : (h + 1) * BLK, :] = src[rows, lanes]

    def chunk(c):
        return pl.ds(pl.multiple_of(c * CHUNK, CHUNK), CHUNK)

    def first_phase(group, carry):
        rows_of(q_s, qg, group)
        rows_of(o_s, og, group)
        gather(rk, kg, group)

        def score(c, top):
            s = lax.dot_general(
                kg[chunk(c), :], qg[...], (((1,), (1,)), ((), ())),
                preferred_element_type=jnp.float32,
            )
            e_s[group, chunk(c), :] = s
            return jnp.maximum(top, jnp.max(s, axis=0, keepdims=True))

        top = lax.fori_loop(
            0, CHUNKS, score, jnp.full((1, ROWS), -jnp.inf, jnp.float32), unroll=UNROLL
        )

        def exponent(c, total):
            e = jnp.exp2((e_s[group, chunk(c), :] - top) * EXP2_SCALE)
            e_s[group, chunk(c), :] = e
            return total + jnp.sum(e, axis=0, keepdims=True)

        total = lax.fori_loop(
            0, CHUNKS, exponent, jnp.zeros((1, ROWS), jnp.float32), unroll=UNROLL
        )
        inverse = 1.0 / total
        inv_s[group] = inverse

        def value_terms(c, carry):
            p = (e_s[group, chunk(c), :] * inverse).astype(jnp.bfloat16)
            dv = jnp.dot(p, og[...], preferred_element_type=jnp.float32)
            n = CHUNK // BLK
            terms[pl.ds(group * TOPK + c * n, n)] = dv.astype(jnp.bfloat16).reshape(n, BLK, HD)
            return carry

        return lax.fori_loop(0, CHUNKS, value_terms, carry, unroll=UNROLL)

    def second_phase(group, carry):
        rows_of(q_s, qg, group)
        rows_of(o_s, og, group)
        gather(rk, kg, group)
        gather(rv, vg, group)

        def d_prob(c, delta):
            dp = lax.dot_general(
                vg[chunk(c), :], og[...], (((1,), (1,)), ((), ())),
                preferred_element_type=jnp.float32,
            )
            dp_s[chunk(c), :] = dp
            return delta + jnp.sum(e_s[group, chunk(c), :] * dp, axis=0, keepdims=True)

        delta = lax.fori_loop(
            0, CHUNKS, d_prob, jnp.zeros((1, ROWS), jnp.float32), unroll=UNROLL
        )
        inverse = inv_s[group]
        delta = delta * inverse
        dq_acc[...] = jnp.zeros_like(dq_acc)

        def key_terms(c, carry):
            p = e_s[group, chunk(c), :] * inverse
            ds = (p * (dp_s[chunk(c), :] - delta)).astype(jnp.bfloat16)
            dk = jnp.dot(ds, qg[...], preferred_element_type=jnp.float32) * SCALE
            n = CHUNK // BLK
            terms[pl.ds(group * TOPK + c * n, n)] = dk.astype(jnp.bfloat16).reshape(n, BLK, HD)
            dq_acc[...] += lax.dot_general(
                ds, kg[chunk(c), :], (((0,), (0,)), ((), ())),
                preferred_element_type=jnp.float32,
            )
            return carry

        lax.fori_loop(0, CHUNKS, key_terms, 0, unroll=UNROLL)
        b, g = group // KVH, group % KVH
        rows = pl.ds(pl.multiple_of(b * BLK, BLK), BLK)
        for h in range(GROUP):
            lanes = pl.ds(pl.multiple_of((g * GROUP + h) * HD, HD), HD)
            dq_s[rows, lanes] = dq_acc[h * BLK : (h + 1) * BLK, :] * SCALE
        return carry

    def back_copy(send, got, index, device):
        return pltpu.make_async_remote_copy(
            src_ref=send.at[pl.ds(CAP * (device[0] * 16 + device[1]), CAP)],
            dst_ref=got.at[pl.ds(CAP * me, CAP)],
            send_sem=send_sem.at[index],
            recv_sem=recv_sem.at[index],
            device_id=device,
            device_id_type=MESH,
        )

    def backward(send, got, index):
        def body(turn, carry):
            devices = peers(turn)
            for a, b in devices:
                for c in range(CAP):
                    send[(a * 16 + b) * CAP + c] = terms[pick_of[c, a * 16 + b]]
            for n, device in enumerate(devices):

                @pl.when(((turn > 0) | (n > 0)) & (device[0] * 16 + device[1] < VALID))
                def _():
                    back_copy(send, got, index, device).start()

            return carry

        lax.fori_loop(0, ROUNDS, body, 0)

        @pl.when(me < VALID)
        def _():
            own = pl.ds(CAP * me, CAP)
            pltpu.make_async_copy(send.at[own], got.at[own], own_sem.at[index - 2]).start()

    def wait_backward(send, got, index):
        @pl.when(me < VALID)
        def _():
            own = pl.ds(CAP * me, CAP)
            pltpu.make_async_copy(send.at[own], got.at[own], own_sem.at[index - 2]).wait()
            wait_bytes(got.at[pl.ds(0, (DEVICES - 1) * CAP)], recv_sem.at[index])
            wait_bytes(send.at[pl.ds(0, SLOTS - CAP)], send_sem.at[index])

        @pl.when(me >= VALID)
        def _():
            wait_bytes(send.at[pl.ds(0, SLOTS)], send_sem.at[index])

    def wait_sent(send, index):
        @pl.when(me < VALID)
        def _():
            wait_bytes(send.at[pl.ds(0, (DEVICES - 1) * CAP)], send_sem.at[index])

    for move in moves:
        move.wait()
    wait_bytes(kl, load_sem.at[0])
    pl.semaphore_wait(barrier, DEVICES - 1)
    forward(kl, sendk, rk, 0)
    wait_bytes(vl, load_sem.at[1])
    forward(vl, sendv, rv, 1)
    load_q.wait()
    load_o.wait()
    wait_forward(rk, 0)
    lax.fori_loop(0, SETS, first_phase, 0)
    wait_sent(sendk, 0)
    backward(sendk, gv_hbm, 2)
    wait_forward(rv, 1)
    lax.fori_loop(0, SETS, second_phase, 0)
    wait_sent(sendv, 1)
    backward(sendv, gk_hbm, 3)
    store_dq = pltpu.make_async_copy(dq_s, dq_hbm, load_sem.at[2])
    store_dq.start()
    wait_backward(sendk, gv_hbm, 2)
    wait_backward(sendv, gk_hbm, 3)
    store_dq.wait()


def exchange(picks, queries, keys, values, d_out):
    anywhere = pl.BlockSpec(memory_space=pl.ANY)
    half, full = jnp.bfloat16, jnp.float32
    table = jax.ShapeDtypeStruct((CAP, DEVICES), jnp.int32)
    back = jax.ShapeDtypeStruct((DEVICES * CAP, BLK, HD), half)
    return pl.pallas_call(
        exchange_kernel,
        out_shape=(jax.ShapeDtypeStruct((QB_DEV * BLK, H * HD), full), back, back, table),
        in_specs=[anywhere] * 5,
        out_specs=[anywhere] * 4,
        scratch_shapes=[
            pltpu.VMEM((DEVICES, PICKS), jnp.int32),
            pltpu.VMEM((CAP, DEVICES), jnp.int32),
            pltpu.VMEM((CAP, DEVICES), jnp.int32),
            pltpu.VMEM((1, PICKS), jnp.int32),
            pltpu.SMEM((CAP, DEVICES), jnp.int32),
            pltpu.SMEM((CAP, DEVICES), jnp.int32),
            pltpu.SMEM((1, PICKS), jnp.int32),
            pltpu.VMEM((TILES, BLK, HD), half),
            pltpu.VMEM((TILES, BLK, HD), half),
            pltpu.VMEM((DEVICES * CAP, BLK, HD), half),
            pltpu.VMEM((DEVICES * CAP, BLK, HD), half),
            pltpu.VMEM((SLOTS, BLK, HD), half),
            pltpu.VMEM((SLOTS, BLK, HD), half),
            pltpu.VMEM((QB_DEV * BLK, H * HD), half),
            pltpu.VMEM((QB_DEV * BLK, H * HD), half),
            pltpu.VMEM((SETS, KEYS, ROWS), full),
            pltpu.VMEM((SETS, 1, ROWS), full),
            pltpu.VMEM((KEYS, ROWS), full),
            pltpu.VMEM((KEYS, HD), half),
            pltpu.VMEM((KEYS, HD), half),
            pltpu.VMEM((ROWS, HD), half),
            pltpu.VMEM((ROWS, HD), half),
            pltpu.VMEM((PICKS, BLK, HD), half),
            pltpu.VMEM((ROWS, HD), full),
            pltpu.VMEM((QB_DEV * BLK, H * HD), full),
            pltpu.SemaphoreType.DMA((8,)),
            pltpu.SemaphoreType.DMA((4,)),
            pltpu.SemaphoreType.DMA((4,)),
            pltpu.SemaphoreType.DMA((2,)),
        ],
        compiler_params=pltpu.CompilerParams(
            collective_id=0, has_side_effects=True, vmem_limit_bytes=62 * MIB
        ),
    )(picks, queries, keys, values, d_out)


FOLD = 32
STEPS = DEVICES * CAP // FOLD


def collect_kernel(
    tile_of, gk, gv, dq_hbm, dq_out, dk_out, dv_out, dk, dk2, dv, dv2, dq, sems
):
    step = pl.program_id(0)
    load = pltpu.make_async_copy(dq_hbm, dq, sems.at[2])
    store = pltpu.make_async_copy(dq, dq_out, sems.at[3])

    @pl.when(step == 0)
    def _():
        load.start()
        for total in (dk, dk2, dv, dv2):
            total[...] = jnp.zeros_like(total)

    @pl.when(step == STEPS // 2)
    def _():
        load.wait()
        store.start()

    def add(i, carry):
        device = step * (FOLD // CAP) + i
        tile, tile2 = tile_of[0, device], tile_of[1, device]
        dk[tile] += gk[CAP * i].astype(jnp.float32)
        dk2[tile2] += gk[CAP * i + 1].astype(jnp.float32)
        dv[tile] += gv[CAP * i].astype(jnp.float32)
        dv2[tile2] += gv[CAP * i + 1].astype(jnp.float32)
        return carry

    lax.fori_loop(0, FOLD // CAP, add, 0, unroll=4)

    @pl.when(step == STEPS - 1)
    def _():
        def put(t, carry):
            rows = pl.ds(pl.multiple_of(t // KVH * BLK, BLK), BLK)
            lanes = pl.ds(pl.multiple_of(t % KVH * HD, HD), HD)
            dk[t] += dk2[t]
            dv[t] += dv2[t]
            pltpu.make_async_copy(dk.at[t], dk_out.at[rows, lanes], sems.at[0]).start()
            pltpu.make_async_copy(dv.at[t], dv_out.at[rows, lanes], sems.at[1]).start()
            return carry

        lax.fori_loop(0, TILES, put, 0)
        pltpu.make_async_copy(dk_out, dk_out, sems.at[0]).wait()
        pltpu.make_async_copy(dv_out, dv_out, sems.at[1]).wait()
        store.wait()


def collect(tile_of, gk, gv, d_queries):
    full = jnp.float32
    shape = jax.ShapeDtypeStruct((KB_DEV * BLK, KVH * HD), full)
    part = pl.BlockSpec((FOLD, BLK, HD), lambda i: (i, 0, 0))
    anywhere = pl.BlockSpec(memory_space=pl.ANY)
    return pl.pallas_call(
        collect_kernel,
        grid=(STEPS,),
        out_shape=(jax.ShapeDtypeStruct(d_queries.shape, full), shape, shape),
        in_specs=[pl.BlockSpec(memory_space=pltpu.SMEM), part, part, anywhere],
        out_specs=[anywhere] * 3,
        scratch_shapes=[pltpu.VMEM((TILES + 1, BLK, HD), full)] * 4
        + [pltpu.VMEM(d_queries.shape, full), pltpu.SemaphoreType.DMA((4,))],
        compiler_params=pltpu.CompilerParams(vmem_limit_bytes=62 * MIB),
    )(tile_of, gk, gv, d_queries)


def body(queries, keys, values, d_out, selection):
    picks = selection.reshape(DEVICES, PICKS)
    d_queries, gk, gv, tile_of = exchange(picks, queries, keys, values, d_out)
    return collect(tile_of, gk, gv, d_queries)


def solution(mesh):
    rows = P(("cx", "cy"), None)
    return jax.shard_map(
        body,
        mesh=mesh,
        in_specs=(rows, rows, rows, rows, P()),
        out_specs=(rows, rows, rows),
        check_vma=False,
    )
```

profile of v0, /device:TPU:19, one launch (start us, length us, event | category | flops | bytes accessed | tf_op | source)
XLA Modules:
  0.0 229.5 jit_solution(7149617720318480718)
XLA Ops:
  0.6 1.2 copy.9
  1.8 1.1 reshape.9.picks_hbm
  2.9 216.7 %shard_map.76 = (f32[192,4096]{1,0:T(8,128)}, bf16[256,64,128]{2,1,0:T(8,128)(2,1)}, bf16[256,64,128]{2,1,0:T(8,128)(2,1)}, s32[2,128]{1,0:T(2,128)}) custom-call(s32[128,192]{1,0:T(8,128)} %reshape.9.picks_hbm, bf16[192,4096]{1,0:T(8,128)(2,1)} %q_hbm.1, bf16[1024,512]{1,0:T(8,128)(2,1)} %k_hbm.1, bf16[1024,512]{1,0:T(8,128)(2,1)} %v_hbm.1, ...), custom_call_target="tpu_custom_call" | custom-call | tf_op jit(solution)/shard_map/pallas_call | solution.py:335
  219.6 9.9 %shard_map.77 = (f32[192,4096]{1,0:T(8,128)}, f32[1024,512]{1,0:T(8,128)}, f32[1024,512]{1,0:T(8,128)}) custom-call(s32[2,128]{1,0:T(2,128)} %get-tuple-element.7.tile_of, bf16[256,64,128]{2,1,0:T(8,128)(2,1)} %get-tuple-element.8.gk, bf16[256,64,128]{2,1,0:T(8,128)(2,1)} %get-tuple-element.9.gv, f32[192,4096]{1,0:T(8,128)} %get-tuple-element.10.dq_hbm), custom_call_target="tpu_custom_call" | custom-call | tf_op jit(solution)/shard_map/pallas_call | solution.py:432
where the time goes:
time: 230 us; the launch traced here: 229 us
  Pallas kernels  227 us (99%)
    pallas_call x1, Pallas kernels, exchange(): pl.pallas_call(exchange_kernel, out_shape=(jax.ShapeDtypeStruct((QB_DEV *...  217 us
    pallas_call x1, Pallas kernels, collect(): pl.pallas_call(collect_kernel, grid=(STEPS,), out_shape=(jax.ShapeDtypeSt...  9.85 us

commit v1 on v0

--- a/solution.py
+++ b/solution.py
@@ -65,12 +65,13 @@
 ):
     cx, cy = lax.axis_index("cx"), lax.axis_index("cy")
     me = cx * 16 + cy
-    at_x = [(cy + a) % 4 for a in range(4)]
-    at_z = [(cy // 4 + b) % 4 * 4 for b in range(4)]
+    sign = 1 + 2 * (cx % 2)
+    at_x = [(cy + a * sign) % 4 for a in range(4)]
+    at_z = [(cy // 4 + b * sign) % 4 * 4 for b in range(4)]
 
     def peers(turn):
         core = (cx + turn // 4) % 2
-        y = [(cx // 2 + turn % 4 + e) % 4 * 2 + core for e in range(4)]
+        y = [(cx // 2 + (turn % 4 + e) * sign) % 4 * 2 + core for e in range(4)]
         return [(y[(a + b) % 4], at_z[(a + b) % 4] + at_x[a]) for a, b in STRIDES]
 
     def load_tiles(src, dst, sem):
@@ -379,64 +380,84 @@
 
 
 def collect_kernel(
-    tile_of, gk, gv, dq_hbm, dq_out, dk_out, dv_out, dk, dk2, dv, dv2, dq, sems
+    tile_of, gk_hbm, gv_hbm, dq_hbm, dq_out, dk_out, dv_out,
+    gk, gv, dk, dk2, dv, dv2, dq, load_sem, sems,
 ):
-    step = pl.program_id(0)
-    load = pltpu.make_async_copy(dq_hbm, dq, sems.at[2])
-    store = pltpu.make_async_copy(dq, dq_out, sems.at[3])
-
-    @pl.when(step == 0)
-    def _():
-        load.start()
-        for total in (dk, dk2, dv, dv2):
-            total[...] = jnp.zeros_like(total)
-
-    @pl.when(step == STEPS // 2)
-    def _():
-        load.wait()
-        store.start()
-
-    def add(i, carry):
-        device = step * (FOLD // CAP) + i
-        tile, tile2 = tile_of[0, device], tile_of[1, device]
-        dk[tile] += gk[CAP * i].astype(jnp.float32)
-        dk2[tile2] += gk[CAP * i + 1].astype(jnp.float32)
-        dv[tile] += gv[CAP * i].astype(jnp.float32)
-        dv2[tile2] += gv[CAP * i + 1].astype(jnp.float32)
+    def load(step):
+        part = pl.ds(pl.multiple_of(step * FOLD, FOLD), FOLD)
+        return (
+            pltpu.make_async_copy(gk_hbm.at[part], gk.at[part], load_sem.at[0, step]),
+            pltpu.make_async_copy(gv_hbm.at[part], gv.at[part], load_sem.at[1, step]),
+        )
+
+    for step in range(STEPS):
+        for copy in load(step):
+            copy.start()
+    load_dq = pltpu.make_async_copy(dq_hbm, dq, sems.at[2])
+    store_dq = pltpu.make_async_copy(dq, dq_out, sems.at[3])
+    load_dq.start()
+    for part in (dk, dk2, dv, dv2):
+        part[...] = jnp.zeros_like(part)
+
+    def fold(step, carry):
+        for copy in load(step):
+            copy.wait()
+
+        def add(i, carry):
+            device = step * (FOLD // CAP) + i
+            slot = device * CAP
+            tile, tile2 = tile_of[0, device], tile_of[1, device]
+            dk[tile] += gk[slot].astype(jnp.float32)
+            dk2[tile2] += gk[slot + 1].astype(jnp.float32)
+            dv[tile] += gv[slot].astype(jnp.float32)
+            dv2[tile2] += gv[slot + 1].astype(jnp.float32)
+            return carry
+
+        return lax.fori_loop(0, FOLD // CAP, add, carry, unroll=4)
+
+    lax.fori_loop(0, STEPS, fold, 0)
+    load_dq.wait()
+    store_dq.start()
+
+    def put(t):
+        rows = pl.ds(pl.multiple_of(t // KVH * BLK, BLK), BLK)
+        lanes = pl.ds(pl.multiple_of(t % KVH * HD, HD), HD)
+        pltpu.make_async_copy(dk.at[t], dk_out.at[rows, lanes], sems.at[0]).start()
+        pltpu.make_async_copy(dv.at[t], dv_out.at[rows, lanes], sems.at[1]).start()
+
+    def total(t, carry):
+        dk[t] += dk2[t]
+        dv[t] += dv2[t]
+
+        @pl.when(t > 0)
+        def _():
+            put(t - 1)
+
         return carry
 
-    lax.fori_loop(0, FOLD // CAP, add, 0, unroll=4)
-
-    @pl.when(step == STEPS - 1)
-    def _():
-        def put(t, carry):
-            rows = pl.ds(pl.multiple_of(t // KVH * BLK, BLK), BLK)
-            lanes = pl.ds(pl.multiple_of(t % KVH * HD, HD), HD)
-            dk[t] += dk2[t]
-            dv[t] += dv2[t]
-            pltpu.make_async_copy(dk.at[t], dk_out.at[rows, lanes], sems.at[0]).start()
-            pltpu.make_async_copy(dv.at[t], dv_out.at[rows, lanes], sems.at[1]).start()
-            return carry
-
-        lax.fori_loop(0, TILES, put, 0)
-        pltpu.make_async_copy(dk_out, dk_out, sems.at[0]).wait()
-        pltpu.make_async_copy(dv_out, dv_out, sems.at[1]).wait()
-        store.wait()
+    lax.fori_loop(0, TILES, total, 0)
+    put(TILES - 1)
+    pltpu.make_async_copy(dk_out, dk_out, sems.at[0]).wait()
+    pltpu.make_async_copy(dv_out, dv_out, sems.at[1]).wait()
+    store_dq.wait()
 
 
 def collect(tile_of, gk, gv, d_queries):
-    full = jnp.float32
+    half, full = jnp.bfloat16, jnp.float32
     shape = jax.ShapeDtypeStruct((KB_DEV * BLK, KVH * HD), full)
-    part = pl.BlockSpec((FOLD, BLK, HD), lambda i: (i, 0, 0))
     anywhere = pl.BlockSpec(memory_space=pl.ANY)
     return pl.pallas_call(
         collect_kernel,
-        grid=(STEPS,),
         out_shape=(jax.ShapeDtypeStruct(d_queries.shape, full), shape, shape),
-        in_specs=[pl.BlockSpec(memory_space=pltpu.SMEM), part, part, anywhere],
+        in_specs=[pl.BlockSpec(memory_space=pltpu.SMEM)] + [anywhere] * 3,
         out_specs=[anywhere] * 3,
-        scratch_shapes=[pltpu.VMEM((TILES + 1, BLK, HD), full)] * 4
-        + [pltpu.VMEM(d_queries.shape, full), pltpu.SemaphoreType.DMA((4,))],
+        scratch_shapes=[pltpu.VMEM(gk.shape, half)] * 2
+        + [pltpu.VMEM((TILES + 1, BLK, HD), full)] * 4
+        + [
+            pltpu.VMEM(d_queries.shape, full),
+            pltpu.SemaphoreType.DMA((2, STEPS)),
+            pltpu.SemaphoreType.DMA((4,)),
+        ],
         compiler_params=pltpu.CompilerParams(vmem_limit_bytes=62 * MIB),
     )(tile_of, gk, gv, d_queries)
 

time: 230 us -> 220 us (0.957)
  Pallas kernels: 227 us -> 214 us
    pallas_call x1, Pallas kernels: 217 us -> 206 us  [exchange(): pl.pallas_call(exchange_kernel, out_shape=(jax.ShapeDtypeStruct((QB_DEV *...]
where the time goes in v1:
time: 220 us; the launch traced here: 217 us
  Pallas kernels  214 us (97%)
  local copies, waits for them, and re-layouts  2.27 us (1%)
    pallas_call x1, Pallas kernels, exchange(): pl.pallas_call(exchange_kernel, out_shape=(jax.ShapeDtypeStruct((QB_DEV *...  206 us
    pallas_call x1, Pallas kernels, collect(): pl.pallas_call(collect_kernel, out_shape=(jax.ShapeDtypeStruct(d_queries....  8.15 us

profile of v1, /device:TPU:19, one launch (start us, length us, event | category | flops | bytes accessed | tf_op | source)
XLA Modules:
  0.0 217.2 jit_solution(11107667291144980259)
XLA Ops:
  0.6 1.2 copy.9
  1.8 1.1 reshape.9.picks_hbm
  2.9 206.1 %shard_map.76 = (f32[192,4096]{1,0:T(8,128)}, bf16[256,64,128]{2,1,0:T(8,128)(2,1)}, bf16[256,64,128]{2,1,0:T(8,128)(2,1)}, s32[2,128]{1,0:T(2,128)}) custom-call(s32[128,192]{1,0:T(8,128)} %reshape.9.picks_hbm, bf16[192,4096]{1,0:T(8,128)(2,1)} %q_hbm.1, bf16[1024,512]{1,0:T(8,128)(2,1)} %k_hbm.1, bf16[1024,512]{1,0:T(8,128)(2,1)} %v_hbm.1, ...), custom_call_target="tpu_custom_call" | custom-call | tf_op jit(solution)/shard_map/pallas_call | solution.py:336
  209.0 8.1 %shard_map.77 = (f32[192,4096]{1,0:T(8,128)}, f32[1024,512]{1,0:T(8,128)}, f32[1024,512]{1,0:T(8,128)}) custom-call(s32[2,128]{1,0:T(2,128)} %get-tuple-element.7.tile_of, bf16[256,64,128]{2,1,0:T(8,128)(2,1)} %get-tuple-element.8.gk_hbm, bf16[256,64,128]{2,1,0:T(8,128)(2,1)} %get-tuple-element.9.gv_hbm, f32[192,4096]{1,0:T(8,128)} %get-tuple-element.10.dq_hbm), custom_call_target="tpu_custom_call" | custom-call | tf_op jit(solution)/shard_map/pallas_call | solution.py:449

commit v2 on v1

--- a/solution.py
+++ b/solution.py
@@ -51,7 +51,7 @@
     pick_of[1:2, :] = jnp.max(jnp.where(held, position, 0), axis=0, keepdims=True)
 
 
-STRIDES = [(a, b) for b in range(4) for a in range(4)]
+STRIDES = [(0, 0)] + [(a, b) for b in (2, 1, 3, 0) for a in (2, 1, 3, 0)][:-1]
 ROUNDS = DEVICES // len(STRIDES)
 
 

time: 220 us -> 211 us (0.959)
  Pallas kernels: 214 us -> 205 us
    pallas_call x1, Pallas kernels: 206 us -> 197 us  [exchange(): pl.pallas_call(exchange_kernel, out_shape=(jax.ShapeDtypeStruct((QB_DEV *...]
where the time goes in v2:
time: 211 us; the launch traced here: 208 us
  Pallas kernels  205 us (97%)
  local copies, waits for them, and re-layouts  2.27 us (1%)
    pallas_call x1, Pallas kernels, exchange(): pl.pallas_call(exchange_kernel, out_shape=(jax.ShapeDtypeStruct((QB_DEV *...  197 us
    pallas_call x1, Pallas kernels, collect(): pl.pallas_call(collect_kernel, out_shape=(jax.ShapeDtypeStruct(d_queries....  8.15 us

profile of v2, /device:TPU:19, one launch (start us, length us, event | category | flops | bytes accessed | tf_op | source)
XLA Modules:
  0.0 207.9 jit_solution(6781413324628770051)
XLA Ops:
  0.6 1.2 copy.9
  1.8 1.1 reshape.9.picks_hbm
  2.9 196.8 %shard_map.76 = (f32[192,4096]{1,0:T(8,128)}, bf16[256,64,128]{2,1,0:T(8,128)(2,1)}, bf16[256,64,128]{2,1,0:T(8,128)(2,1)}, s32[2,128]{1,0:T(2,128)}) custom-call(s32[128,192]{1,0:T(8,128)} %reshape.9.picks_hbm, bf16[192,4096]{1,0:T(8,128)(2,1)} %q_hbm.1, bf16[1024,512]{1,0:T(8,128)(2,1)} %k_hbm.1, bf16[1024,512]{1,0:T(8,128)(2,1)} %v_hbm.1, ...), custom_call_target="tpu_custom_call" | custom-call | tf_op jit(solution)/shard_map/pallas_call | solution.py:336
  199.8 8.1 %shard_map.77 = (f32[192,4096]{1,0:T(8,128)}, f32[1024,512]{1,0:T(8,128)}, f32[1024,512]{1,0:T(8,128)}) custom-call(s32[2,128]{1,0:T(2,128)} %get-tuple-element.7.tile_of, bf16[256,64,128]{2,1,0:T(8,128)(2,1)} %get-tuple-element.8.gk_hbm, bf16[256,64,128]{2,1,0:T(8,128)(2,1)} %get-tuple-element.9.gv_hbm, f32[192,4096]{1,0:T(8,128)} %get-tuple-element.10.dq_hbm), custom_call_target="tpu_custom_call" | custom-call | tf_op jit(solution)/shard_map/pallas_call | solution.py:449
